TPU v7x, 32 devices: a whole 2x2x4 slice. The times are simulated.
32 devices in a mesh: gx: 2 (over x), gy: 4 (over z), gz: 4 (over y, core).
Axes of the slice: x: 2, y: 2, z: 4, core: 2. Of those that a mesh axis runs over, the one named last changes fastest.
Arguments:
- density: float32 [192, 256, 512], P('gz', 'gx', 'gy'), may hold values from 0.0005 to 0.01
- shear_offsets: int32 [2, 192], P(None, 'gz'), may hold values from 0 to 48, as said below
- shear_fractions: float32 [2, 192], P(None, 'gz'), may hold values from 0 to 1
- flat_field: float32 [256, 512], P(('gx', 'gz'), 'gy'), may hold values from 0.5 to 1.5
Outputs:
- normalized: float32 [256, 512], P(('gx', 'gz'), 'gy')
Inputs may be any that keep to these rules, and one draw needn't show every extreme that they name: `shear_offsets`: in each row, the shift never falls from one slice to the next and rises by at most 1; it is 0 or 1 at slice 0 and exactly 48 at the last slice.
All inputs are finite; a program needn't handle non-finite values.
Results may differ from a plain program's by a relative error of at most 0.0003.
Values sent between devices are 32-bit elements; how exact they have to be, the bound alone decides.
A program may use at most 64 MiB of HBM per device.

v0:
```python
import jax
import jax.numpy as jnp
from jax import lax
from jax.sharding import PartitionSpec as P


def passed_along(value, axis, steps):
    count = lax.axis_size(axis)
    initial, last = (max(0, -steps), min(count, count - steps))
    return lax.ppermute(value, axis, [(source, source + steps) for source in range(initial, last)])


def shards(density, shear_offsets, shear_fractions, flat_field):
    slices, tile_rows, tile_cols = density.shape
    center = slices * lax.axis_size("gz") // 8
    margin = center + 1
    used_cols = tile_cols + 2 * margin
    padded_cols = (used_cols + 127) // 128 * 128
    screen = jnp.zeros((tile_rows + 2 * margin, padded_cols), jnp.float32)
    source_cols = lax.broadcasted_iota(jnp.int32, (tile_cols, padded_cols), 0)
    target_cols = lax.broadcasted_iota(jnp.int32, (tile_cols, padded_cols), 1)

    def march_slab(slice_index, carry):
        slab = lax.dynamic_index_in_dim(density, slice_index, 0, keepdims=False)
        offset_pair = lax.dynamic_index_in_dim(shear_offsets, slice_index, 1, keepdims=False)
        frac_pair = lax.dynamic_index_in_dim(shear_fractions, slice_index, 1, keepdims=False)
        start_u = offset_pair[0] - center + margin
        start_v = offset_pair[1] - center + margin
        frac_u = frac_pair[0]
        frac_v = frac_pair[1]
        placed = source_cols + start_v
        placing = jnp.where(target_cols == placed, 1.0 - frac_v, 0.0) + jnp.where(
            target_cols == placed + 1, frac_v, 0.0
        )
        spread_cols = jnp.dot(
            slab, placing, precision=lax.Precision.HIGHEST, preferred_element_type=jnp.float32
        )
        spread = jnp.pad(spread_cols * (1.0 - frac_u), ((0, 1), (0, 0)))
        spread = spread + jnp.pad(spread_cols * frac_u, ((1, 0), (0, 0)))
        window = lax.dynamic_slice(carry, (start_u, jnp.int32(0)), (tile_rows + 1, padded_cols))
        return lax.dynamic_update_slice(carry, window + spread, (start_u, jnp.int32(0)))

    screen = lax.fori_loop(0, slices, march_slab, screen)
    screen = screen[:, :used_cols]
    band = screen[margin : margin + tile_rows]
    from_lower = passed_along(screen[margin + tile_rows :], "gx", 1)
    from_upper = passed_along(screen[:margin], "gx", -1)
    band = band.at[:margin].add(from_lower)
    band = band.at[tile_rows - margin :].add(from_upper)
    tile_total = band[:, margin : margin + tile_cols]
    from_left = passed_along(band[:, margin + tile_cols :], "gy", 1)
    from_right = passed_along(band[:, :margin], "gy", -1)
    tile_total = tile_total.at[:, :margin].add(from_left)
    tile_total = tile_total.at[:, tile_cols - margin :].add(from_right)
    integral = lax.psum_scatter(tile_total, "gz", scatter_dimension=0, tiled=True)
    detected = flat_field * jnp.exp(-integral)
    largest = lax.pmax(jnp.max(detected), ("gx", "gy", "gz"))
    return detected / largest


def solution(mesh):
    in_specs = (P("gz", "gx", "gy"), P(None, "gz"), P(None, "gz"), P(("gx", "gz"), "gy"))
    out_specs = P(("gx", "gz"), "gy")
    return jax.shard_map(shards, mesh=mesh, in_specs=in_specs, out_specs=out_specs, check_vma=False)
```

profile of v0, /device:TPU:0, one launch (start us, length us, event | category | flops | bytes accessed | tf_op | source)
XLA Modules:
  0.0 526.9 jit_solution(2166855292301451949)
XLA Ops:
  6.6 428.3 %while.24 = (s32[]{:T(128)}, f32[178,256]{1,0:T(8,128)S(1)}, s32[2,48]{1,0:T(2,128)}, f32[48,128,128]{2,1,0:T(8,128)}, f32[2,48]{1,0:T(2,128)}, /*index=5*/s32[]...) while((s32[]{:T(128)}, f32[178,256]{1,0:T(8,128)S(1)}, ...), condition=%wide.region_1.2_spmd.clone.clone, body=%wide.region_0.1_spmd.clone.clone.sunk | while | flops 50692612 | bytes 1120527 | solution.py:43
  11.1 2.4 broadcast_multiply_fusion.3
  20.0 2.4 broadcast_multiply_fusion.3
  28.9 2.4 broadcast_multiply_fusion.3
  37.8 2.4 broadcast_multiply_fusion.3
  46.8 2.4 broadcast_multiply_fusion.3
  55.7 2.4 broadcast_multiply_fusion.3
  64.6 2.4 broadcast_multiply_fusion.3
  73.5 2.4 broadcast_multiply_fusion.3
  82.5 2.4 broadcast_multiply_fusion.3
  91.4 2.4 broadcast_multiply_fusion.3
  100.3 2.4 broadcast_multiply_fusion.3
  109.2 2.4 broadcast_multiply_fusion.3
  127.1 2.4 broadcast_multiply_fusion.3
  136.0 2.4 broadcast_multiply_fusion.3
  145.0 2.4 broadcast_multiply_fusion.3
  153.9 2.4 broadcast_multiply_fusion.3
  162.8 2.4 broadcast_multiply_fusion.3
  171.7 2.4 broadcast_multiply_fusion.3
  180.7 2.4 broadcast_multiply_fusion.3
  189.6 2.4 broadcast_multiply_fusion.3
  198.5 2.4 broadcast_multiply_fusion.3
  207.4 2.4 broadcast_multiply_fusion.3
  216.4 2.4 broadcast_multiply_fusion.3
  225.3 2.4 broadcast_multiply_fusion.3
  234.2 2.4 broadcast_multiply_fusion.3
  243.1 2.4 broadcast_multiply_fusion.3
  252.1 2.4 broadcast_multiply_fusion.3
  261.0 2.4 broadcast_multiply_fusion.3
  269.9 2.4 broadcast_multiply_fusion.3
  278.8 2.4 broadcast_multiply_fusion.3
  296.7 2.4 broadcast_multiply_fusion.3
  305.6 2.4 broadcast_multiply_fusion.3
  314.6 2.4 broadcast_multiply_fusion.3
  323.5 2.4 broadcast_multiply_fusion.3
  332.4 2.4 broadcast_multiply_fusion.3
  341.3 2.4 broadcast_multiply_fusion.3
  350.3 2.4 broadcast_multiply_fusion.3
  359.2 2.4 broadcast_multiply_fusion.3
  368.1 2.4 broadcast_multiply_fusion.3
  403.8 2.4 broadcast_multiply_fusion.3
  430.5 2.4 broadcast_multiply_fusion.3
  434.9 4.9 collective-permute-start
  443.1 4.1 collective-permute-done.1
  447.5 3.5 collective-permute-start.2
  454.2 3.7 collective-permute-done.3
  459.2 18.1 %reduce-scatter.2.cloned.1.call-done = f32[32,128]{1,0:T(8,128)} async-done(((f32[128,128]{1,0:T(8,128)}), f32[32,128]{1,0:T(8,128)}) %reduce-scatter.2.cloned.1.call-update) | async-done | bytes 16400 | tf_op jit(solution)/shard_map/reduce_scatter | solution.py:55
  478.7 39.5 %pmax.7 = f32[]{:T(128)} all-reduce(f32[]{:T(128)} %fusion.19), channel_id=1, replica_groups=mesh['gx'=2,'gy'=4,'gz'=4] {'gx','gy','gz'}, use_global_device_ids=true, to_apply=%region_5.6 | all-reduce | flops 1 | bytes 8 | tf_op jit(solution)/shard_map/pmax | solution.py:57
  (321 shorter events, 194.7 us)
Async XLA Ops:
  6.5 470.8 %reduce-scatter.2.cloned.1.call-start = ((), (), s32[]{:S(2)}) async-start(), calls=%async_computation.1 | async-start | bytes 81920 | tf_op jit(solution)/shard_map/reduce_scatter | solution.py:55
  6.6 470.8 %copy-start.1 = (f32[32,128]{1,0:T(8,128)S(1)}, f32[32,128]{1,0:T(8,128)}, u32[]{:S(2)}) copy-start(f32[32,128]{1,0:T(8,128)} %param.17) | copy-start | bytes 49156
  434.9 6.5 %collective-permute-start = (f32[25,178]{1,0:T(8,128)S(1)}, f32[25,178]{1,0:T(8,128)S(1)}, u32[]{:S(2)}, u32[]{:S(2)}) collective-permute-start(f32[25,178]{1,0:T(8,128)S(1)} %slice.162), channel_id=1, source_target_pairs={{0,16},{1,17},{2,18},{3,19},{4,20},{5,21},{6,22},{7,23},{8,24},{9,... | collective-permute-start | bytes 53408 | tf_op jit(solution)/shard_map/ppermute | solution.py:10
  441.4 5.8 %collective-permute-start.1 = (f32[25,178]{1,0:T(8,128)S(1)}, f32[25,178]{1,0:T(8,128)S(1)}, u32[]{:S(2)}, u32[]{:S(2)}) collective-permute-start(f32[25,178]{1,0:T(8,128)S(1)} %get-tuple-element.364), channel_id=1, source_target_pairs={{16,0},{17,1},{18,2},{19,3},{20,4},{21,5},{22,6},{23,7},{24,8},{25... | collective-permute-start | bytes 53408 | tf_op jit(solution)/shard_map/ppermute | solution.py:10
  447.5 5.5 %collective-permute-start.2 = (f32[128,25]{1,0:T(8,128)S(1)}, f32[128,25]{1,0:T(8,128)S(1)}, u32[]{:S(2)}, u32[]{:S(2)}) collective-permute-start(f32[128,25]{1,0:T(8,128)S(1)} %get-tuple-element.367), channel_id=1, source_target_pairs={{0,4},{4,8},{8,12},{1,5},{5,9},{9,13},{2,6},{6,10},{10,14},{3,7},{... | collective-permute-start | bytes 38408 | tf_op jit(solution)/shard_map/ppermute | solution.py:10
  451.8 6.2 %collective-permute-start.3 = (f32[128,25]{1,0:T(8,128)S(1)}, f32[128,25]{1,0:T(8,128)S(1)}, u32[]{:S(2)}, u32[]{:S(2)}) collective-permute-start(f32[128,25]{1,0:T(8,128)S(1)} %get-tuple-element.366), channel_id=1, source_target_pairs={{4,0},{8,4},{12,8},{5,1},{9,5},{13,9},{6,2},{10,6},{14,10},{7,3},{... | collective-permute-start | bytes 38408 | tf_op jit(solution)/shard_map/ppermute | solution.py:10
  458.6 0.6 copy-start
Sparse Core Ops, SparseCore 0:
  459.4 17.9 reduce-scatter.1
where the time goes:
time: 534 us; the launch traced here: 527 us
  local copies, waits for them, and re-layouts  167 us (31%)
  loops' own time  148 us (28%)
  matrix products  114 us (21%)
  blocking collectives  39.5 us (7%)
  waiting for transfers between devices  27.5 us (5%)
  between operations  13.5 us (3%)
  starting transfers between devices  10.9 us (2%)
  other arithmetic  6.63 us (1%)
    another operation x1, loops' own time, shards(): screen = lax.fori_loop(0, slices, march_slab, screen)  148 us
    dot_general x48, matrix products, march_slab(): jnp.dot(slab, placing, precision=lax.Precision.HIGHEST, preferred_element...  114 us
    pmax x1, blocking collectives, shards(): largest = lax.pmax(jnp.max(detected), ('gx', 'gy', 'gz'))  39.5 us
    dynamic_update_slice x48, local copies, waits for them, and re-layouts, march_slab(): lax.dynamic_update_slice(carry, window + spread, (start_u, jnp.int32(0)))  37.4 us
    dynamic_slice x48, local copies, waits for them, and re-layouts, march_slab(): lax.dynamic_index_in_dim(shear_fractions, slice_index, 1, keepdims=False)  36.3 us
    dynamic_slice x48, local copies, waits for them, and re-layouts, march_slab(): lax.dynamic_index_in_dim(shear_offsets, slice_index, 1, keepdims=False)  36.2 us
    slice x48, local copies, waits for them, and re-layouts, march_slab(): frac_u = frac_pair[0]  28.7 us
    slice x48, local copies, waits for them, and re-layouts, march_slab(): start_u = offset_pair[0] - center + margin  26.2 us
  transfers between devices with their start and end apart: 5, of which 4 were waited for; matrix products, arithmetic and copies ran while one was open for 0% of the time, Pallas kernels for 0%

commit v1 on v0

v1 whole, which is shorter than its diff:
```python
import functools

import jax
import jax.numpy as jnp
from jax import lax
from jax.experimental import pallas as pl
from jax.experimental.pallas import tpu as pltpu
from jax.sharding import PartitionSpec as P

MESH = pl.DeviceIdType.MESH


def plan(tile_rows, tile_cols, slices, nx, ny, nz):
    center = slices * nz // 8
    height = tile_rows // nz
    below = -(-center // height)
    above = -(-(center + 1) // height)
    pad = (max(below, above) * height + center + 8) // 8 * 8
    pad = max(pad, 8)
    packed = 2 * center + 1 <= tile_cols
    return center, height, below, above, pad, packed


def kernel(
    nx, ny, nz, offsets, fracs, flat, density, out,
    volume, staged, landed, total, peak, peaks,
    in_sem, send_sem, recv_sem, peak_send, peak_recv,
):
    slices, tile_rows, tile_cols = density.shape
    center, height, below, above, pad, packed = plan(tile_rows, tile_cols, slices, nx, ny, nz)
    stride = tile_rows + pad
    devices = nx * ny * nz
    ix, iy, iz = lax.axis_index("gx"), lax.axis_index("gy"), lax.axis_index("gz")
    me = (ix * ny + iy) * nz + iz

    def place(index):
        return (index // (ny * nz), (index // nz) % ny, index % nz)

    def fetch(z):
        return pltpu.make_async_copy(
            density.at[z], volume.at[pl.ds(pad + z * stride, tile_rows)], in_sem.at[z]
        )

    @pl.loop(0, slices)
    def _(z):
        fetch(z).start()

    barrier = pltpu.get_barrier_semaphore()

    @pl.loop(1, devices)
    def _(k):
        pl.semaphore_signal(
            barrier, inc=1, device_id=place((me + k) % devices), device_id_type=MESH
        )

    volume[pl.ds(0, pad), :] = jnp.zeros((pad, tile_cols), jnp.float32)

    @pl.loop(0, slices)
    def _(z):
        start = pl.multiple_of(pad + z * stride + tile_rows, 8)
        volume[pl.ds(start, pad), :] = jnp.zeros((pad, tile_cols), jnp.float32)

    @pl.loop(0, slices)
    def _(z):
        fetch(z).wait()
        base = pl.multiple_of(pad + z * stride, 8)
        here = volume[pl.ds(base, tile_rows + 8), :]
        before = volume[pl.ds(base - 1, tile_rows + 8), :]
        mixed = here + fracs[0, z] * (before - here)
        turn = lax.rem(offsets[1, z] - center + tile_cols, tile_cols)
        volume[pl.ds(base, tile_rows + 8), :] = pltpu.roll(mixed, turn, 1)

    pl.semaphore_wait(barrier, devices - 1)

    lane = lax.broadcasted_iota(jnp.int32, (height, tile_cols), 1)
    edges = 1 if packed else 2

    def messages(block):
        step = (block + nz) // nz - 1
        row = block - step * nz
        source = (step + 3) % 3
        found = []
        for side, (shift, tile) in enumerate(((0, 0), (1, 1), (-1, edges))):
            exists = (iy + shift >= 0) & (iy + shift < ny)
            if side == 0:
                exists = (step != 0) | (row != iz)
            copy = pltpu.make_async_remote_copy(
                src_ref=staged.at[block + below, tile],
                dst_ref=landed.at[source, side, iz],
                send_sem=send_sem.at[block + below, side],
                recv_sem=recv_sem.at[source, side, iz],
                device_id=(ix + step, iy + shift, row),
                device_id_type=MESH,
            )
            found.append((exists, copy))
        return found

    def project(block):
        zero = jnp.zeros((height, tile_cols), jnp.float32)
        first = pad + block * height + center

        def add(z, sums):
            whole, late, *parts = sums
            value = volume[pl.ds(first + z * stride - offsets[0, z], height), :]
            moved = value * fracs[1, z]
            turn = offsets[1, z] - center
            right = lane < turn
            left = lane >= tile_cols + turn
            masks = (right | left,) if packed else (right, left)
            grown = [whole + value, late + moved]
            for n, mask in enumerate(masks):
                grown.append(parts[2 * n] + jnp.where(mask, value, 0.0))
                grown.append(parts[2 * n + 1] + jnp.where(mask, moved, 0.0))
            return tuple(grown)

        unroll = next(n for n in (8, 4, 2, 1) if slices % n == 0)

        def several(group, sums):
            for n in range(unroll):
                sums = add(group * unroll + n, sums)
            return sums

        whole, late, *parts = lax.fori_loop(
            0, slices // unroll, several, (zero,) * (2 + 2 * edges)
        )
        for n in range(edges):
            whole = whole - parts[2 * n]
            late = late - parts[2 * n + 1]
        turned = pltpu.roll(late, 1, 1)
        ends = [pltpu.roll(parts[2 * n + 1], 1, 1) for n in range(edges)]
        begin = lane == 0
        staged[block + below, 0] = whole - late + jnp.where(begin, ends[-1], turned)
        staged[block + below, 1] = parts[0] - parts[1] + jnp.where(begin, turned, ends[0])
        if not packed:
            staged[block + below, 2] = parts[2] - parts[3] + jnp.where(begin, 0.0, ends[1])
        for exists, copy in messages(block):
            @pl.when(exists)
            def _():
                copy.start()

    def own(k):
        cores = 2 if nz % 2 == 0 else 1
        chips = nz // cores
        chip, core = iz // cores, iz % cores
        return ((chip + 1 + k // cores) % chips) * cores + (core + 1 + k) % cores

    @pl.when(ix > 0)
    def _():
        @pl.loop(0, below)
        def _(k):
            project(k - below)

    @pl.when(ix < nx - 1)
    def _():
        @pl.loop(0, above)
        def _(k):
            project(nz + k)

    @pl.loop(0, nz)
    def _(k):
        project(own(k))

    total[...] = staged[iz + below, 0]
    for side, beside in ((0, None), (1, iy > 0), (2, iy < ny - 1)):
        for source, within in ((1, (ix > 0) & (iz < above)), (2, (ix < nx - 1) & (iz >= nz - below)), (0, None)):
            def collect(j):
                slot = landed.at[source, side, j]
                pltpu.make_async_remote_copy(
                    src_ref=slot, dst_ref=slot, send_sem=send_sem.at[0, 0],
                    recv_sem=recv_sem.at[source, side, j],
                    device_id=(ix, iy, iz), device_id_type=MESH,
                ).wait_recv()
                value = slot[...]
                if side == 1:
                    value = jnp.where(lane <= center, value, 0.0)
                if side == 2:
                    value = jnp.where(lane >= tile_cols - center, value, 0.0)
                total[...] += value

            def gather():
                @pl.loop(0, nz)
                def _(j):
                    if source == 0 and side == 0:
                        pl.when(j != iz)(lambda: collect(j))
                    else:
                        collect(j)

            cond = [c for c in (beside, within) if c is not None]
            if cond:
                pl.when(functools.reduce(lambda a, b: a & b, cond))(gather)
            else:
                gather()

    detected = flat[...] * jnp.exp(-total[...])
    peak[...] = jnp.max(detected, axis=0, keepdims=True)

    def tell(k):
        return pltpu.make_async_remote_copy(
            src_ref=peak,
            dst_ref=peaks.at[me],
            send_sem=peak_send,
            recv_sem=peak_recv,
            device_id=place((me + k) % devices),
            device_id_type=MESH,
        )

    @pl.loop(1, devices)
    def _(k):
        tell(k).start()

    peaks[me] = peak[...]
    others = peaks.at[pl.ds(0, devices - 1)]
    pltpu.make_async_copy(others, others, peak_recv).wait()
    out[...] = detected / jnp.max(peaks[...])
    pltpu.make_async_copy(others, others, peak_send).wait()

    def drain(block):
        for exists, copy in messages(block):
            @pl.when(exists)
            def _():
                copy.wait_send()

    @pl.when(ix > 0)
    def _():
        @pl.loop(0, below)
        def _(k):
            drain(k - below)

    @pl.when(ix < nx - 1)
    def _():
        @pl.loop(0, above)
        def _(k):
            drain(nz + k)

    @pl.loop(0, nz)
    def _(k):
        drain(k)


def solution(mesh):
    nx, ny, nz = mesh.shape["gx"], mesh.shape["gy"], mesh.shape["gz"]

    def shards(density, shear_offsets, shear_fractions, flat_field):
        slices, tile_rows, tile_cols = density.shape
        center, height, below, above, pad, packed = plan(tile_rows, tile_cols, slices, nx, ny, nz)
        blocks = below + nz + above
        devices = nx * ny * nz
        block = (height, tile_cols)
        return pl.pallas_call(
            functools.partial(kernel, nx, ny, nz),
            out_shape=jax.ShapeDtypeStruct(block, jnp.float32),
            in_specs=[
                pl.BlockSpec(memory_space=pltpu.SMEM),
                pl.BlockSpec(memory_space=pltpu.SMEM),
                pl.BlockSpec(memory_space=pltpu.VMEM),
                pl.BlockSpec(memory_space=pl.ANY),
            ],
            out_specs=pl.BlockSpec(memory_space=pltpu.VMEM),
            scratch_shapes=[
                pltpu.VMEM((pad + slices * (tile_rows + pad), tile_cols), jnp.float32),
                pltpu.VMEM((blocks, 2 if packed else 3) + block, jnp.float32),
                pltpu.VMEM((3, 3, nz) + block, jnp.float32),
                pltpu.VMEM(block, jnp.float32),
                pltpu.VMEM((1, tile_cols), jnp.float32),
                pltpu.VMEM((devices, 1, tile_cols), jnp.float32),
                pltpu.SemaphoreType.DMA((slices,)),
                pltpu.SemaphoreType.DMA((blocks, 3)),
                pltpu.SemaphoreType.DMA((3, 3, nz)),
                pltpu.SemaphoreType.DMA,
                pltpu.SemaphoreType.DMA,
            ],
            compiler_params=pltpu.CompilerParams(collective_id=0, has_side_effects=True),
        )(shear_offsets, shear_fractions, flat_field, density)

    in_specs = (P("gz", "gx", "gy"), P(None, "gz"), P(None, "gz"), P(("gx", "gz"), "gy"))
    out_specs = P(("gx", "gz"), "gy")
    return jax.shard_map(shards, mesh=mesh, in_specs=in_specs, out_specs=out_specs, check_vma=False)
```

time: 534 us -> 22.9 us (0.04); the launches traced: 527 us -> 22.6 us
  local copies, waits for them, and re-layouts: 167 us -> 1.32 us
  loops' own time: 148 us -> 0 us
  matrix products: 114 us -> 0 us
  blocking collectives: 39.5 us -> 0 us
  waiting for transfers between devices: 27.5 us -> 0 us
  Pallas kernels: 0 us -> 21.2 us
  between operations: 13.5 us -> 0.01 us
  starting transfers between devices: 10.9 us -> 0 us
  other arithmetic: 6.63 us -> 0 us
    another operation x1 -> x0, loops' own time: 148 us -> none  [shards(): screen = lax.fori_loop(0, slices, march_slab, screen)]
    dot_general x48 -> x0, matrix products: 114 us -> none  [march_slab(): jnp.dot(slab, placing, precision=lax.Precision.HIGHEST, preferred_element...]
    dynamic_slice x96 -> x0, local copies, waits for them, and re-layouts: 72.5 us -> none  [the longest x48 36.3 us: march_slab(): lax.dynamic_index_in_dim(shear_fractions, slice_index, 1, keepdims=False)]
    slice x100 -> x0, local copies, waits for them, and re-layouts: 55.2 us -> none  [the longest x48 28.7 us: march_slab(): frac_u = frac_pair[0]]
    pmax x1 -> x0, blocking collectives: 39.5 us -> none  [shards(): largest = lax.pmax(jnp.max(detected), ('gx', 'gy', 'gz'))]
    dynamic_update_slice x48 -> x0, local copies, waits for them, and re-layouts: 37.4 us -> none  [march_slab(): lax.dynamic_update_slice(carry, window + spread, (start_u, jnp.int32(0)))]
    pallas_call x0 -> x1, Pallas kernels: none -> 21.2 us  [shards(): pl.pallas_call(functools.partial(kernel, nx, ny, nz), out_shape=jax.Shape...]
    reduce_scatter x1 -> x0, waiting for transfers between devices: 18.1 us -> none  [shards(): lax.psum_scatter(tile_total, 'gz', scatter_dimension=0, tiled=True)]
  transfers between devices with their start and end apart: 5 -> 0, of which waited for: 4 -> 0; matrix products, arithmetic and copies ran while one was open for 0% -> 0% of each run, Pallas kernels for 0% -> 0%
where the time goes in v1:
time: 22.9 us; the launch traced here: 22.6 us
  Pallas kernels  21.2 us (93%)
  local copies, waits for them, and re-layouts  1.32 us (6%)
    pallas_call x1, Pallas kernels, shards(): pl.pallas_call(functools.partial(kernel, nx, ny, nz), out_shape=jax.Shape...  21.2 us
    unnamed x1, local copies, waits for them, and re-layouts  1.32 us

profile of v1, /device:TPU:0, one launch (start us, length us, event | category | flops | bytes accessed | tf_op | source)
XLA Modules:
  0.0 22.6 jit_solution(8017601402985364612)
XLA Ops:
  0.0 21.2 %shard_map.46 = f32[32,128]{1,0:T(8,128)} custom-call(s32[2,48]{1,0:T(2,128)} %offsets.1, f32[2,48]{1,0:T(2,128)} %fracs.1, f32[32,128]{1,0:T(8,128)} %flat.1, f32[48,128,128]{2,1,0:T(8,128)} %density.1), custom_call_target="tpu_custom_call" | custom-call | tf_op jit(solution)/shard_map/pallas_call | solution.py:249
  21.2 1.3 %copy.6 = f32[32,128]{1,0:T(8,128)} copy(f32[32,128]{1,0:T(8,128)} %shard_map.46) | data formatting | bytes 32768

commit v2 on v1

--- a/solution.py
+++ b/solution.py
@@ -22,9 +22,9 @@
 
 
 def kernel(
-    nx, ny, nz, offsets, fracs, flat, density, out,
-    volume, staged, landed, total, peak, peaks,
-    in_sem, send_sem, recv_sem, peak_send, peak_recv,
+    nx, ny, nz, offsets_in, fracs_in, flat_in, density, out,
+    offsets, fracs, flat, arrived, volume, staged, landed, total, peak, peaks,
+    small_sem, in_sem, send_sem, recv_sem, peak_send, peak_recv,
 ):
     slices, tile_rows, tile_cols = density.shape
     center, height, below, above, pad, packed = plan(tile_rows, tile_cols, slices, nx, ny, nz)
@@ -36,14 +36,27 @@
     def place(index):
         return (index // (ny * nz), (index // nz) % ny, index % nz)
 
-    def fetch(z):
+    group = next(n for n in (8, 4, 2, 1) if slices % n == 0)
+    small = [
+        pltpu.make_async_copy(source, target, small_sem.at[n])
+        for n, (source, target) in enumerate(
+            ((offsets_in, offsets), (fracs_in, fracs), (flat_in, flat))
+        )
+    ]
+    for copy in small:
+        copy.start()
+
+    def fetch(n):
+        first = n * group
         return pltpu.make_async_copy(
-            density.at[z], volume.at[pl.ds(pad + z * stride, tile_rows)], in_sem.at[z]
-        )
-
-    @pl.loop(0, slices)
-    def _(z):
-        fetch(z).start()
+            density.at[pl.ds(first, group)],
+            arrived.at[pl.ds(first, group), pl.ds(8, tile_rows)],
+            in_sem.at[n],
+        )
+
+    @pl.loop(0, slices // group)
+    def _(n):
+        fetch(n).start()
 
     barrier = pltpu.get_barrier_semaphore()
 
@@ -59,16 +72,23 @@
     def _(z):
         start = pl.multiple_of(pad + z * stride + tile_rows, 8)
         volume[pl.ds(start, pad), :] = jnp.zeros((pad, tile_cols), jnp.float32)
-
-    @pl.loop(0, slices)
-    def _(z):
-        fetch(z).wait()
-        base = pl.multiple_of(pad + z * stride, 8)
-        here = volume[pl.ds(base, tile_rows + 8), :]
-        before = volume[pl.ds(base - 1, tile_rows + 8), :]
-        mixed = here + fracs[0, z] * (before - here)
-        turn = lax.rem(offsets[1, z] - center + tile_cols, tile_cols)
-        volume[pl.ds(base, tile_rows + 8), :] = pltpu.roll(mixed, turn, 1)
+        arrived[z, pl.ds(0, 8), :] = jnp.zeros((8, tile_cols), jnp.float32)
+        arrived[z, pl.ds(8 + tile_rows, 8), :] = jnp.zeros((8, tile_cols), jnp.float32)
+
+    for copy in small:
+        copy.wait()
+
+    @pl.loop(0, slices // group)
+    def _(n):
+        fetch(n).wait()
+        for k in range(group):
+            z = n * group + k
+            here = arrived[z, pl.ds(8, tile_rows + 8), :]
+            before = arrived[z, pl.ds(7, tile_rows + 8), :]
+            mixed = here + fracs[0, z] * (before - here)
+            turn = lax.rem(offsets[1, z] - center + tile_cols, tile_cols)
+            base = pl.multiple_of(pad + z * stride, 8)
+            volume[pl.ds(base, tile_rows + 8), :] = pltpu.roll(mixed, turn, 1)
 
     pl.semaphore_wait(barrier, devices - 1)
 
@@ -250,19 +270,21 @@
             functools.partial(kernel, nx, ny, nz),
             out_shape=jax.ShapeDtypeStruct(block, jnp.float32),
             in_specs=[
-                pl.BlockSpec(memory_space=pltpu.SMEM),
-                pl.BlockSpec(memory_space=pltpu.SMEM),
-                pl.BlockSpec(memory_space=pltpu.VMEM),
                 pl.BlockSpec(memory_space=pl.ANY),
-            ],
+            ] * 4,
             out_specs=pl.BlockSpec(memory_space=pltpu.VMEM),
             scratch_shapes=[
+                pltpu.SMEM(shear_offsets.shape, jnp.int32),
+                pltpu.SMEM(shear_fractions.shape, jnp.float32),
+                pltpu.VMEM(block, jnp.float32),
+                pltpu.VMEM((slices, tile_rows + 16, tile_cols), jnp.float32),
                 pltpu.VMEM((pad + slices * (tile_rows + pad), tile_cols), jnp.float32),
                 pltpu.VMEM((blocks, 2 if packed else 3) + block, jnp.float32),
                 pltpu.VMEM((3, 3, nz) + block, jnp.float32),
                 pltpu.VMEM(block, jnp.float32),
                 pltpu.VMEM((1, tile_cols), jnp.float32),
                 pltpu.VMEM((devices, 1, tile_cols), jnp.float32),
+                pltpu.SemaphoreType.DMA((3,)),
                 pltpu.SemaphoreType.DMA((slices,)),
                 pltpu.SemaphoreType.DMA((blocks, 3)),
                 pltpu.SemaphoreType.DMA((3, 3, nz)),

time: 22.9 us -> 19.8 us (0.86)
  Pallas kernels: 21.2 us -> 18.2 us
    pallas_call x1, Pallas kernels: 21.2 us -> 18.2 us  [shards(): pl.pallas_call(functools.partial(kernel, nx, ny, nz), out_shape=jax.Shape...]
where the time goes in v2:
time: 19.8 us; the launch traced here: 19.5 us
  Pallas kernels  18.2 us (92%)
  local copies, waits for them, and re-layouts  1.32 us (7%)
    pallas_call x1, Pallas kernels, shards(): pl.pallas_call(functools.partial(kernel, nx, ny, nz), out_shape=jax.Shape...  18.2 us
    unnamed x1, local copies, waits for them, and re-layouts  1.32 us

profile of v2, /device:TPU:0, one launch (start us, length us, event | category | flops | bytes accessed | tf_op | source)
XLA Modules:
  0.0 19.5 jit_solution(3178662834951470731)
XLA Ops:
  0.0 18.2 %shard_map.46 = f32[32,128]{1,0:T(8,128)} custom-call(s32[2,48]{1,0:T(2,128)} %offsets_in.1, f32[2,48]{1,0:T(2,128)} %fracs_in.1, f32[32,128]{1,0:T(8,128)} %flat_in.1, f32[48,128,128]{2,1,0:T(8,128)} %density.1), custom_call_target="tpu_custom_call" | custom-call | tf_op jit(solution)/shard_map/pallas_call | solution.py:269
  18.2 1.3 %copy.6 = f32[32,128]{1,0:T(8,128)} copy(f32[32,128]{1,0:T(8,128)} %shard_map.46) | data formatting | bytes 32768

commit v3 on v2

--- a/solution.py
+++ b/solution.py
@@ -60,7 +60,7 @@
 
     barrier = pltpu.get_barrier_semaphore()
 
-    @pl.loop(1, devices)
+    @pl.loop(1, devices, unroll=devices <= 32)
     def _(k):
         pl.semaphore_signal(
             barrier, inc=1, device_id=place((me + k) % devices), device_id_type=MESH
@@ -89,8 +89,6 @@
             turn = lax.rem(offsets[1, z] - center + tile_cols, tile_cols)
             base = pl.multiple_of(pad + z * stride, 8)
             volume[pl.ds(base, tile_rows + 8), :] = pltpu.roll(mixed, turn, 1)
-
-    pl.semaphore_wait(barrier, devices - 1)
 
     lane = lax.broadcasted_iota(jnp.int32, (height, tile_cols), 1)
     edges = 1 if packed else 2
@@ -153,10 +151,9 @@
         staged[block + below, 1] = parts[0] - parts[1] + jnp.where(begin, turned, ends[0])
         if not packed:
             staged[block + below, 2] = parts[2] - parts[3] + jnp.where(begin, 0.0, ends[1])
+    def send(block):
         for exists, copy in messages(block):
-            @pl.when(exists)
-            def _():
-                copy.start()
+            pl.when(exists)(copy.start)
 
     def own(k):
         cores = 2 if nz % 2 == 0 else 1
@@ -164,21 +161,29 @@
         chip, core = iz // cores, iz % cores
         return ((chip + 1 + k // cores) % chips) * cores + (core + 1 + k) % cores
 
-    @pl.when(ix > 0)
-    def _():
-        @pl.loop(0, below)
+    def border(act):
+        @pl.when(ix > 0)
+        def _():
+            pl.loop(0, below)(lambda k: act(k - below))
+
+        @pl.when(ix < nx - 1)
+        def _():
+            pl.loop(0, above)(lambda k: act(nz + k))
+
+    early = nz // 2
+    border(project)
+    if early:
+        pl.loop(0, early)(lambda k: project(own(k)))
+    pl.semaphore_wait(barrier, devices - 1)
+    border(send)
+    if early:
+        pl.loop(0, early)(lambda k: send(own(k)))
+
+    if early < nz:
+        @pl.loop(early, nz)
         def _(k):
-            project(k - below)
-
-    @pl.when(ix < nx - 1)
-    def _():
-        @pl.loop(0, above)
-        def _(k):
-            project(nz + k)
-
-    @pl.loop(0, nz)
-    def _(k):
-        project(own(k))
+            project(own(k))
+            send(own(k))
 
     total[...] = staged[iz + below, 0]
     for side, beside in ((0, None), (1, iy > 0), (2, iy < ny - 1)):
@@ -198,7 +203,7 @@
                 total[...] += value
 
             def gather():
-                @pl.loop(0, nz)
+                @pl.loop(0, nz, unroll=nz <= 4)
                 def _(j):
                     if source == 0 and side == 0:
                         pl.when(j != iz)(lambda: collect(j))
@@ -224,9 +229,16 @@
             device_id_type=MESH,
         )
 
-    @pl.loop(1, devices)
+    far = devices // 2
+
+    @pl.loop(0, devices - far, unroll=devices <= 32)
     def _(k):
-        tell(k).start()
+        tell(far + k).start()
+
+    if far > 1:
+        @pl.loop(1, far, unroll=devices <= 32)
+        def _(k):
+            tell(k).start()
 
     peaks[me] = peak[...]
     others = peaks.at[pl.ds(0, devices - 1)]
@@ -236,25 +248,10 @@
 
     def drain(block):
         for exists, copy in messages(block):
-            @pl.when(exists)
-            def _():
-                copy.wait_send()
-
-    @pl.when(ix > 0)
-    def _():
-        @pl.loop(0, below)
-        def _(k):
-            drain(k - below)
-
-    @pl.when(ix < nx - 1)
-    def _():
-        @pl.loop(0, above)
-        def _(k):
-            drain(nz + k)
-
-    @pl.loop(0, nz)
-    def _(k):
-        drain(k)
+            pl.when(exists)(copy.wait_send)
+
+    border(drain)
+    pl.loop(0, nz)(drain)
 
 
 def solution(mesh):

time: 19.8 us -> 18.9 us (0.955)
  Pallas kernels: 18.2 us -> 17.3 us
    pallas_call x1, Pallas kernels: 18.2 us -> 17.3 us  [shards(): pl.pallas_call(functools.partial(kernel, nx, ny, nz), out_shape=jax.Shape...]
where the time goes in v3:
time: 18.9 us; the launch traced here: 18.7 us
  Pallas kernels  17.3 us (92%)
  local copies, waits for them, and re-layouts  1.32 us (7%)
    pallas_call x1, Pallas kernels, shards(): pl.pallas_call(functools.partial(kernel, nx, ny, nz), out_shape=jax.Shape...  17.3 us
    unnamed x1, local copies, waits for them, and re-layouts  1.32 us

profile of v3, /device:TPU:0, one launch (start us, length us, event | category | flops | bytes accessed | tf_op | source)
XLA Modules:
  0.0 18.7 jit_solution(7482841101845707767)
XLA Ops:
  0.0 17.3 %shard_map.46 = f32[32,128]{1,0:T(8,128)} custom-call(s32[2,48]{1,0:T(2,128)} %offsets_in.1, f32[2,48]{1,0:T(2,128)} %fracs_in.1, f32[32,128]{1,0:T(8,128)} %flat_in.1, f32[48,128,128]{2,1,0:T(8,128)} %density.1), custom_call_target="tpu_custom_call" | custom-call | tf_op jit(solution)/shard_map/pallas_call | solution.py:266
  17.4 1.3 %copy.6 = f32[32,128]{1,0:T(8,128)} copy(f32[32,128]{1,0:T(8,128)} %shard_map.46) | data formatting | bytes 32768

commit v4 on v3

--- a/solution.py
+++ b/solution.py
@@ -131,7 +131,7 @@
                 grown.append(parts[2 * n + 1] + jnp.where(mask, moved, 0.0))
             return tuple(grown)
 
-        unroll = next(n for n in (8, 4, 2, 1) if slices % n == 0)
+        unroll = next(n for n in (16, 8, 4, 2, 1) if slices % n == 0)
 
         def several(group, sums):
             for n in range(unroll):

time: 18.9 us -> 18.8 us (level)
  no operation moved by 1% of the time
where the time goes in v4:
time: 18.8 us; the launch traced here: 18.6 us
  Pallas kernels  17.2 us (91%)
  local copies, waits for them, and re-layouts  1.32 us (7%)
    pallas_call x1, Pallas kernels, shards(): pl.pallas_call(functools.partial(kernel, nx, ny, nz), out_shape=jax.Shape...  17.2 us
    unnamed x1, local copies, waits for them, and re-layouts  1.32 us

profile of v4, /device:TPU:0, one launch (start us, length us, event | category | flops | bytes accessed | tf_op | source)
XLA Modules:
  0.0 18.6 jit_solution(13053310279409559988)
XLA Ops:
  0.0 17.2 %shard_map.46 = f32[32,128]{1,0:T(8,128)} custom-call(s32[2,48]{1,0:T(2,128)} %offsets_in.1, f32[2,48]{1,0:T(2,128)} %fracs_in.1, f32[32,128]{1,0:T(8,128)} %flat_in.1, f32[48,128,128]{2,1,0:T(8,128)} %density.1), custom_call_target="tpu_custom_call" | custom-call | tf_op jit(solution)/shard_map/pallas_call | solution.py:266
  17.3 1.3 %copy.6 = f32[32,128]{1,0:T(8,128)} copy(f32[32,128]{1,0:T(8,128)} %shard_map.46) | data formatting | bytes 32768
